TPU v7x, 32 devices: a whole 2x2x4 slice. The times are simulated.
32 devices in a mesh: member: 4 (over y, x), lat: 2 (over core), lon: 4 (over z).
Axes of the slice: x: 2, y: 2, z: 4, core: 2. Of those that a mesh axis runs over, the one named last changes fastest.
Arguments:
- ice_flux: float32 [8, 64, 8, 512], P(('member', 'lat'), 'lon'), parts along dimension 0, may hold values from 0.5 to 1.5
- ice_frac: float32 [8, 64, 512], P(('member', 'lat'), 'lon'), parts along dimension 0, may hold values from 0.05 to 1
- ice_mask: int32 [8, 64, 512], P(('member', 'lat'), 'lon'), parts along dimension 0, may hold values 0 or 1
- ice_area: float32 [8, 64, 512], P(('member', 'lat'), 'lon'), parts along dimension 0, may hold values from 0.7 to 44.3
- route: int32 [8, 64], P(('member', 'lat'), 'lon'), parts along dimension 0, may hold values from 0 to 63, as said below
- ocean_area: float32 [512, 512], P(('member', 'lat'), 'lon'), parts along dimension 0, may hold values from 0.7 to 44.3
- ocean_wet: int32 [512, 512], P(('member', 'lat'), 'lon'), parts along dimension 0, may hold values 0 or 1
- exponent: int32 [8], replicated, may hold values from 0 to 3
Outputs:
- ocean_flux: float32 [8, 512, 512], P(None, ('member', 'lat'), 'lon'), parts along dimension 1
- source_total: float32 [32], P('member'), parts along dimension 0
There are 4 independent parts, one for each index of `member`. A program takes and returns all parts, laid end to end along the dimension named above; an argument that names none is the same for every part. Nothing has to cross between parts.
Inputs may be any that keep to these rules, and one draw needn't show every extreme that they name: Within each latitude tile row, route is a permutation of 0 to 63. The 16 entries of one device name, for every longitude tile k that they name (route // 16 == k), exactly 4 blocks of it.
All inputs are finite; a program needn't handle non-finite values. No bound on the sum of `ice_mask` or of `ocean_wet` on one device may be relied on, other than what follows from the above.
Results may differ from a plain program's by a relative error of at most 0.0003.
Values sent between devices are 32-bit elements; how exact they have to be, the bound alone decides.
A program may use at most 64 MiB of HBM per device.

v0:
```python
import functools

import jax
import jax.numpy as jnp
from jax import lax
from jax.experimental import pallas as pl
from jax.experimental.pallas import tpu as pltpu
from jax.sharding import PartitionSpec as P

MESH = pl.DeviceIdType.MESH
quantum = 1024.0
limb_bits = 16
limb_base = 65536.0
lanes = 128


def carry(upper, lower):
    over = jnp.floor(lower * (1.0 / limb_base))
    return upper + over, lower - over * limb_base


def row_limbs(units):
    upper = jnp.sum((units >> limb_bits).astype(jnp.float32), axis=1, keepdims=True)
    lower = jnp.sum((units & 0xFFFF).astype(jnp.float32), axis=1, keepdims=True)
    return carry(upper, lower)


def join(upper, lower):
    return (upper * limb_base + lower) / quantum


def send_steps(count):
    table = []
    for me in range(count):
        near = sorted((p for p in range(count) if p != me), key=lambda p: (abs(p - me), p))
        table.append(near[-1:] + near[:-1])
    return [[row[step] for row in table] for step in range(count - 1)]


def kernel(
    n_lat, n_lon, cap,
    flux_hbm, frac_hbm, mask_hbm, area_hbm, route_hbm, sea_hbm, wet_hbm, exp_hbm,
    ordered, wetf, coefs, total_ref,
    flux, frac, mask, area, sea, wet, inverse, outgoing, received, routes, exps, sums,
    in_sem, route_send, route_recv, bulk_send, bulk_recv, sum_send, sum_recv,
):
    blocks, fields, cells = flux.shape
    rows, width = sea.shape
    band = cells // width
    bits = blocks.bit_length()
    digit = (1 << bits) - 1
    full = cap * n_lon == blocks
    group = n_lat * n_lon
    my_lat = lax.axis_index("lat")
    me = lax.axis_index("lon")

    def peer(offset):
        return {
            "lat": lax.rem(my_lat + offset // n_lon, n_lat),
            "lon": lax.rem(me + offset % n_lon, n_lon),
        }

    loads = [
        pltpu.make_async_copy(src, dst, in_sem.at[i])
        for i, (src, dst) in enumerate((
            (route_hbm, routes.at[pl.ds(0, 1)]), (area_hbm, area), (frac_hbm, frac),
            (mask_hbm, mask), (flux_hbm, flux), (sea_hbm, sea), (wet_hbm, wet), (exp_hbm, exps),
        ))
    ]
    for load in loads:
        load.start()

    barrier = pltpu.get_barrier_semaphore()
    for offset in range(1, group):
        pl.semaphore_signal(barrier, inc=1, device_id=peer(offset), device_id_type=MESH)

    loads[0].wait()

    def digits_of(slot, low, value):
        packed = jnp.int32(0)
        for s in range(blocks):
            r = routes[slot, s]
            hit = (r >= low) & (r < low + blocks)
            packed = jnp.where(hit, (packed << bits) + (value(s, r - low) + 1), packed)
        return [(packed >> (bits * (cap - 1 - c))) & digit for c in range(cap)]

    pl.semaphore_wait(barrier, group - 1)

    if n_lon ** n_lon < 2 ** 31:
        place = 1
        for i in range(n_lon - 1):
            place = place * (1 + (n_lon - 1) * ((me + n_lon - 1 - i) // n_lon))
        steps = [
            sum(t * n_lon ** i for i, t in enumerate(row)) // place % n_lon
            for row in send_steps(n_lon)
        ]
    else:
        steps = [lax.rem(me + d, n_lon) for d in range(1, n_lon)]
    away = [lax.rem(target - me + n_lon, n_lon) for target in steps]

    def lon_copy(src, dst, send, recv, d, target):
        return pltpu.make_async_remote_copy(
            src_ref=src, dst_ref=dst, send_sem=send.at[d - 1], recv_sem=recv.at[d - 1],
            device_id={"lat": my_lat, "lon": target}, device_id_type=MESH,
        )

    route_copies = [
        lon_copy(routes.at[pl.ds(0, 1)], routes.at[pl.ds(d, 1)], route_send, route_recv, d, t)
        for d, t in zip(away, steps)
    ]
    for copy in route_copies:
        copy.start()

    chosen = [
        [jnp.maximum(v - 1, 0) for v in digits_of(0, target * blocks, lambda s, row: s)]
        for target in steps + [me]
    ]
    for load in loads[1:5]:
        load.wait()

    bulk = []
    for step, picks in enumerate(chosen):
        last = step == n_lon - 1
        for c, s in enumerate(picks):
            here = pl.ds(s, 1)
            amount = area[here, :] * frac[here, :] * mask[here, :].astype(jnp.float32)
            block = flux[s] * amount
            if last:
                received[c] = block
            else:
                outgoing[step * cap + c] = block
        if not last:
            d = away[step]
            bulk.append(lon_copy(
                outgoing.at[pl.ds(step * cap, cap)], received.at[pl.ds(d * cap, cap)],
                bulk_send, bulk_recv, d, steps[step],
            ))
            bulk[-1].start()

    def arrival(d):
        here = received.at[pl.ds(d * cap, cap)]
        line = routes.at[pl.ds(d, 1)]
        source = lax.rem(me - d + n_lon, n_lon)
        return (
            lon_copy(line, line, route_send, route_recv, d, source),
            lon_copy(here, here, bulk_send, bulk_recv, d, source),
        )

    source_units = jnp.zeros((fields, width), jnp.int32)
    for s in range(blocks):
        here = pl.ds(s, 1)
        amount = area[here, :] * frac[here, :] * mask[here, :].astype(jnp.float32)
        units = (flux[s] * amount * quantum).astype(jnp.int32)
        for r in range(band):
            source_units += units[:, r * width : (r + 1) * width]

    for load in loads[5:]:
        load.wait()
    wetf[...] = wet[...].astype(jnp.float32)
    inverse[...] = wetf[...] / sea[...]
    area_units = jnp.zeros((8, width), jnp.int32)
    for i in range(rows // 8):
        part = pl.ds(i * 8, 8)
        area_units += (sea[part, :] * wetf[part, :] * quantum).astype(jnp.int32)

    sub = lax.broadcasted_iota(jnp.int32, (8, lanes), 0)
    lane = lax.broadcasted_iota(jnp.int32, (8, lanes), 1)

    def placed(values, first):
        return sum(
            jnp.where(lane == sub + (first + i) * 8, v, 0.0) for i, v in enumerate(values)
        )

    early = placed(row_limbs(source_units) + row_limbs(area_units), 0)
    power = jnp.zeros((8, lanes), jnp.int32)
    power_row = jnp.zeros((1, lanes), jnp.int32)
    for f in range(fields):
        power = jnp.where(sub == f, exps[f], power)
        power_row = jnp.where(lane[:1] == f, exps[f], power_row)
    scaling = jnp.left_shift(jnp.ones_like(power), power).astype(jnp.float32)
    scaling_row = jnp.left_shift(jnp.ones_like(power_row), power_row).astype(jnp.float32)

    low = me * blocks
    slot_of = [jnp.int32(0)] * blocks
    target_units = jnp.zeros((fields, width), jnp.int32)
    near_first = sorted(range(n_lon), key=lambda d: min(d, n_lon - d))
    for d in near_first:
        if d:
            route_arrival, bulk_arrival = arrival(d)
            route_arrival.wait_recv()
        digits = digits_of(d, low, lambda s, row: row)
        for c in range(cap):
            for n in range(blocks):
                slot_of[n] = jnp.where(digits[c] == n + 1, d * cap + c, slot_of[n])
        if d:
            bulk_arrival.wait_recv()
        for c in range(cap):
            row = jnp.maximum(digits[c] - 1, 0)
            for r in range(band):
                cover = wetf[pl.ds(row * band + r, 1), :]
                value = received[d * cap + c, :, r * width : (r + 1) * width]
                units = (cover * value * quantum).astype(jnp.int32)
                if not full:
                    units = units * jnp.minimum(digits[c], 1)
                target_units += units

    mine = jnp.sum(early + placed(row_limbs(target_units), 4), axis=0, keepdims=True)
    sums[pl.ds(0, 1), :] = mine
    sum_copies = []
    for offset in range(1, group):
        copy = pltpu.make_async_remote_copy(
            src_ref=sums.at[pl.ds(0, 1)], dst_ref=sums.at[pl.ds(offset, 1)],
            send_sem=sum_send.at[offset - 1], recv_sem=sum_recv.at[offset - 1],
            device_id=peer(offset), device_id_type=MESH,
        )
        copy.start()
        sum_copies.append(copy)
    for n in range(blocks):
        slot = slot_of[n]
        for r in range(band):
            line = n * band + r
            value = received[slot, :, r * width : (r + 1) * width]
            ordered[pl.ds(line, fields, stride=rows), :] = value * inverse[line : line + 1, :]

    for copy in sum_copies:
        copy.wait_recv()

    whole = jnp.sum(sums[...], axis=0, keepdims=True)

    def taken(i):
        return jnp.sum(jnp.where(lane == sub + i * 8, whole, 0.0), axis=1, keepdims=True)

    source = join(taken(0), taken(1))
    wet_upper, wet_lower = carry(taken(2), taken(3))
    wet_area = join(
        jnp.sum(wet_upper, axis=0, keepdims=True), jnp.sum(wet_lower, axis=0, keepdims=True)
    )
    target = join(taken(4), taken(5))
    coefs[0] = scaling
    coefs[1] = scaling * ((source - target) / wet_area)

    aligned = pltpu.roll(whole, lanes - 8, 1)
    total_ref[...] = join(whole, aligned) * scaling_row

    for copy in sum_copies + route_copies + bulk:
        copy.wait_send()


def finish(ordered, wetf, coefs, total_row, out_hbm, total_ref, out, sems):
    fields = total_ref.shape[0]
    rows = wetf.shape[0]
    copies = []
    for f in range(fields):
        here = pl.ds(f * rows, rows)
        out[here, :] = ordered[here, :] * coefs[0, f : f + 1, :] + wetf[...] * coefs[1, f : f + 1, :]
        copies.append(pltpu.make_async_copy(out.at[here], out_hbm.at[here], sems.at[f]))
        copies[-1].start()
    total_ref[...] = total_row[0, :fields]
    for copy in copies:
        copy.wait()


def solution(mesh):
    n_lat, n_lon = mesh.shape["lat"], mesh.shape["lon"]

    def body(ice_flux, ice_frac, ice_mask, ice_area, route, ocean_area, ocean_wet, exponent):
        blocks, fields, cells = ice_flux.shape[1:]
        rows, width = ocean_area.shape
        cap = max(2, blocks // n_lon)
        group = n_lat * n_lon
        anywhere = pl.BlockSpec(memory_space=pl.ANY)
        vmem = pl.BlockSpec(memory_space=pltpu.VMEM)
        dma = pltpu.SemaphoreType.DMA
        near = pl.pallas_call(
            functools.partial(kernel, n_lat, n_lon, cap),
            out_shape=(
                pltpu.VMEM((fields * rows, width), jnp.float32),
                pltpu.VMEM((rows, width), jnp.float32),
                pltpu.VMEM((2, fields, lanes), jnp.float32),
                pltpu.VMEM((1, lanes), jnp.float32),
            ),
            in_specs=[anywhere] * 8,
            out_specs=(vmem,) * 4,
            scratch_shapes=[
                pltpu.VMEM((blocks, fields, cells), jnp.float32),
                pltpu.VMEM((blocks, cells), jnp.float32),
                pltpu.VMEM((blocks, cells), jnp.int32),
                pltpu.VMEM((blocks, cells), jnp.float32),
                pltpu.VMEM((rows, width), jnp.float32),
                pltpu.VMEM((rows, width), jnp.int32),
                pltpu.VMEM((rows, width), jnp.float32),
                pltpu.VMEM(((n_lon - 1) * cap, fields, cells), jnp.float32),
                pltpu.VMEM((n_lon * cap, fields, cells), jnp.float32),
                pltpu.SMEM((n_lon, blocks), jnp.int32),
                pltpu.SMEM((fields,), jnp.int32),
                pltpu.VMEM((group, lanes), jnp.float32),
                dma((8,)),
                dma((n_lon - 1,)), dma((n_lon - 1,)),
                dma((n_lon - 1,)), dma((n_lon - 1,)),
                dma((group - 1,)), dma((group - 1,)),
            ],
            compiler_params=pltpu.CompilerParams(collective_id=0, has_side_effects=True),
        )(
            ice_flux[0], ice_frac[0], ice_mask[0], ice_area[0],
            route, ocean_area, ocean_wet, exponent,
        )
        flux_out, total = pl.pallas_call(
            finish,
            out_shape=(
                jax.ShapeDtypeStruct((fields * rows, width), jnp.float32),
                jax.ShapeDtypeStruct((fields,), jnp.float32),
            ),
            in_specs=[vmem] * 4,
            out_specs=(anywhere, vmem),
            scratch_shapes=[pltpu.VMEM((fields * rows, width), jnp.float32), dma((fields,))],
        )(*(pltpu.with_memory_space_constraint(x, pltpu.VMEM) for x in near))
        return flux_out.reshape(fields, rows, width), total

    placed = (
        P(("member", "lat"), "lon", None, None),
        P(("member", "lat"), "lon", None),
        P(("member", "lat"), "lon", None),
        P(("member", "lat"), "lon", None),
        P(("member", "lat"), "lon"),
        P(("member", "lat"), "lon"),
        P(("member", "lat"), "lon"),
        P(),
    )
    return jax.shard_map(
        body,
        mesh=mesh,
        in_specs=placed,
        out_specs=(P(None, ("member", "lat"), "lon"), P("member")),
        check_vma=False,
    )
```

profile of v0, /device:TPU:0, one launch (start us, length us, event | category | flops | bytes accessed | tf_op | source)
XLA Modules:
  0.0 18.1 jit_solution(3545388544071018835)
XLA Ops:
  0.6 16.2 %shard_map.95 = (f32[512,128]{1,0:T(8,128)S(1)}, f32[64,128]{1,0:T(8,128)S(1)}, f32[2,8,128]{2,1,0:T(8,128)S(1)}, f32[1,128]{1,0:T(1,128)S(1)}) custom-call(f32[16,8,512]{2,1,0:T(8,128)} %bitcast.5, f32[16,512]{1,0:T(8,128)} %bitcast.6, s32[16,512]{1,0:T(8,128)} %bitcast.7, f32[16,512]{1,0:T(8,128)} %bitcast.8, s32[1,16]{1,0:T(1,128)} %route_hbm.1, ...), custom_call_target="tpu_custom_call" | custom-call | tf_op jit(solution)/shard_map/pallas_call | solution.py:274
  16.8 1.3 %shard_map.96 = (f32[512,128]{1,0:T(8,128)}, f32[8]{0:T(128)}) custom-call(f32[512,128]{1,0:T(8,128)S(1)} %get-tuple-element.8.ordered, f32[64,128]{1,0:T(8,128)S(1)} %get-tuple-element.9.wetf, f32[2,8,128]{2,1,0:T(8,128)S(1)} %get-tuple-element.10.coefs, f32[1,128]{1,0:T(1,128)S(1)} %get-tuple-element.11.total_row), custom_call_target="tpu_custom_call" | custom-call | tf_op jit(solution)/shard_map/pallas_call | solution.py:307
where the time goes:
time: 18.3 us; the launch traced here: 18.1 us
  Pallas kernels  17.5 us (96%)
  between operations  0.64 us (3%)
    pallas_call x1, Pallas kernels, body(): pl.pallas_call(functools.partial(kernel, n_lat, n_lon, cap), out_shape=(p...  16.2 us
    pallas_call x1, Pallas kernels, body(): pl.pallas_call(finish, out_shape=(jax.ShapeDtypeStruct((fields * rows, wi...  1.28 us

commit v1 on v0

--- a/solution.py
+++ b/solution.py
@@ -246,16 +246,17 @@
         copy.wait_send()
 
 
-def finish(ordered, wetf, coefs, total_row, out_hbm, total_ref, out, sems):
-    fields = total_ref.shape[0]
+def finish(ordered, wetf, coefs, total_row, out_hbm, total_hbm, out, total, sems):
+    fields = total.shape[0]
     rows = wetf.shape[0]
-    copies = []
+    total[...] = total_row[0, :fields]
+    copies = [pltpu.make_async_copy(total, total_hbm, sems.at[fields])]
+    copies[0].start()
     for f in range(fields):
         here = pl.ds(f * rows, rows)
         out[here, :] = ordered[here, :] * coefs[0, f : f + 1, :] + wetf[...] * coefs[1, f : f + 1, :]
         copies.append(pltpu.make_async_copy(out.at[here], out_hbm.at[here], sems.at[f]))
         copies[-1].start()
-    total_ref[...] = total_row[0, :fields]
     for copy in copies:
         copy.wait()
 
@@ -311,8 +312,12 @@
                 jax.ShapeDtypeStruct((fields,), jnp.float32),
             ),
             in_specs=[vmem] * 4,
-            out_specs=(anywhere, vmem),
-            scratch_shapes=[pltpu.VMEM((fields * rows, width), jnp.float32), dma((fields,))],
+            out_specs=(anywhere, anywhere),
+            scratch_shapes=[
+                pltpu.VMEM((fields * rows, width), jnp.float32),
+                pltpu.VMEM((fields,), jnp.float32),
+                dma((fields + 1,)),
+            ],
         )(*(pltpu.with_memory_space_constraint(x, pltpu.VMEM) for x in near))
         return flux_out.reshape(fields, rows, width), total
 

time: 18.3 us -> 17.8 us (0.973)
  Pallas kernels: 17.5 us -> 17 us
    pallas_call x1, Pallas kernels: 1.28 us -> 0.78 us  [body(): pl.pallas_call(finish, out_shape=(jax.ShapeDtypeStruct((fields * rows, wi...]
where the time goes in v1:
time: 17.8 us; the launch traced here: 17.6 us
  Pallas kernels  17 us (96%)
  between operations  0.64 us (4%)
    pallas_call x1, Pallas kernels, body(): pl.pallas_call(functools.partial(kernel, n_lat, n_lon, cap), out_shape=(p...  16.2 us
    pallas_call x1, Pallas kernels, body(): pl.pallas_call(finish, out_shape=(jax.ShapeDtypeStruct((fields * rows, wi...  0.78 us

profile of v1, /device:TPU:0, one launch (start us, length us, event | category | flops | bytes accessed | tf_op | source)
XLA Modules:
  0.0 17.6 jit_solution(13292751384596722181)
XLA Ops:
  0.6 16.2 %shard_map.95 = (f32[512,128]{1,0:T(8,128)S(1)}, f32[64,128]{1,0:T(8,128)S(1)}, f32[2,8,128]{2,1,0:T(8,128)S(1)}, f32[1,128]{1,0:T(1,128)S(1)}) custom-call(f32[16,8,512]{2,1,0:T(8,128)} %bitcast.5, f32[16,512]{1,0:T(8,128)} %bitcast.6, s32[16,512]{1,0:T(8,128)} %bitcast.7, f32[16,512]{1,0:T(8,128)} %bitcast.8, s32[1,16]{1,0:T(1,128)} %route_hbm.1, ...), custom_call_target="tpu_custom_call" | custom-call | tf_op jit(solution)/shard_map/pallas_call | solution.py:275
  16.8 0.8 %shard_map.96 = (f32[512,128]{1,0:T(8,128)}, f32[8]{0:T(128)}) custom-call(f32[512,128]{1,0:T(8,128)S(1)} %get-tuple-element.8.ordered, f32[64,128]{1,0:T(8,128)S(1)} %get-tuple-element.9.wetf, f32[2,8,128]{2,1,0:T(8,128)S(1)} %get-tuple-element.10.coefs, f32[1,128]{1,0:T(1,128)S(1)} %get-tuple-element.11.total_row), custom_call_target="tpu_custom_call" | custom-call | tf_op jit(solution)/shard_map/pallas_call | solution.py:308

commit v2 on v1

v2 whole, which is shorter than its diff:
```python
import functools

import jax
import jax.numpy as jnp
from jax import lax
from jax.experimental import pallas as pl
from jax.experimental.pallas import tpu as pltpu
from jax.sharding import PartitionSpec as P

MESH = pl.DeviceIdType.MESH
quantum = 1024.0
limb_bits = 16
limb_base = 65536.0
lanes = 128


def carry(upper, lower):
    over = jnp.floor(lower * (1.0 / limb_base))
    return upper + over, lower - over * limb_base


def row_limbs(units):
    upper = jnp.sum((units >> limb_bits).astype(jnp.float32), axis=1, keepdims=True)
    lower = jnp.sum((units & 0xFFFF).astype(jnp.float32), axis=1, keepdims=True)
    return carry(upper, lower)


def join(upper, lower):
    return (upper * limb_base + lower) / quantum


PLANS = {
    4: (
        (4, 6, 7, 5, 2, 3),
        (4, 6, 7, 0, 1, 5),
        (2, 3, 0, 1, 6, 7),
        (2, 3, 0, 1, 4, 5),
        (2, 4, 6, -8, 5, 3),
        (4, 5, 6, -8, 0, 1),
        (2, 0, 1, 3, 6, 7),
        (2, 0, 1, 3, 4, 5),
    ),
}
EARLY = 3
PARTS = 2


def send_plan(count):
    rows = PLANS.get(count)
    if rows is None:
        rows = [
            [
                target * PARTS + half
                for target in sorted((p for p in range(count) if p != me), key=lambda p: -abs(p - me))
                for half in range(PARTS)
            ]
            for _ in range(2)
            for me in range(count)
        ]
    codes = [[(code if code >= 0 else ~code, code < 0) for code in row] for row in rows]
    return [[(code // PARTS, code % PARTS, hold) for code, hold in row] for row in codes]


def kernel(
    n_lat, n_lon, cap,
    flux_hbm, frac_hbm, mask_hbm, area_hbm, route_hbm, sea_hbm, wet_hbm, exp_hbm,
    ordered, wetf, coefs, total_ref,
    flux, frac, mask, area, sea, wet, inverse, outgoing, received, routes, exps, tally,
    in_sem, route_send, route_recv, bulk_send, bulk_recv, tally_send, early_recv, late_recv, top_in, go,
):
    blocks, fields, cells = flux.shape
    rows, width = sea.shape
    band = cells // width
    bits = blocks.bit_length()
    digit = (1 << bits) - 1
    full = cap * n_lon == blocks
    group = n_lat * n_lon
    piece = cap // PARTS
    my_lat = lax.axis_index("lat")
    me = lax.axis_index("lon")

    def peer(offset):
        return {
            "lat": lax.rem(my_lat + offset // n_lon, n_lat),
            "lon": lax.rem(me + offset % n_lon, n_lon),
        }

    loads = [
        pltpu.make_async_copy(src, dst, in_sem.at[i])
        for i, (src, dst) in enumerate((
            (route_hbm, routes.at[pl.ds(0, 1)]), (area_hbm, area), (frac_hbm, frac),
            (mask_hbm, mask), (flux_hbm, flux), (sea_hbm, sea), (wet_hbm, wet), (exp_hbm, exps),
        ))
    ]
    for load in loads:
        load.start()

    top = n_lon - 1
    barrier = pltpu.get_barrier_semaphore()
    for offset in range(1, n_lat):
        pl.semaphore_signal(barrier, inc=1, device_id=peer(offset * n_lon), device_id_type=MESH)

    @pl.when(me < top)
    def _():
        for offset in range(1, n_lon):
            pl.semaphore_signal(barrier, inc=1, device_id=peer(offset), device_id_type=MESH)

    @pl.when(me == top)
    def _():
        pl.semaphore_wait(barrier, n_lat + n_lon - 2)
        for z in range(top):
            pl.semaphore_signal(
                top_in, inc=1, device_id={"lat": my_lat, "lon": z}, device_id_type=MESH
            )

    loads[0].wait()

    def digits_of(slot, low, value):
        packed = jnp.int32(0)
        for s in range(blocks):
            r = routes[slot, s]
            hit = (r >= low) & (r < low + blocks)
            packed = jnp.where(hit, (packed << bits) + (value(s, r - low) + 1), packed)
        return [(packed >> (bits * (cap - 1 - c))) & digit for c in range(cap)]

    kind = lax.rem(my_lat, 2) if n_lat > 1 else jnp.int32(0)
    place = kind * n_lon + me

    def mine_of(values):
        out = jnp.int32(values[0])
        for z, v in enumerate(values):
            if v != values[0]:
                out = jnp.where(place == z, jnp.int32(v), out)
        return out

    plans = send_plan(n_lon)
    entries = len(plans[0])
    targets = [mine_of([plan[k][0] for plan in plans]) for k in range(entries)]
    halves = [mine_of([plan[k][1] for plan in plans]) for k in range(entries)]
    holds = [[plan[k][2] for plan in plans] for k in range(entries)]
    firsts = [
        [plan[k][0] not in [e[0] for e in plan[:k]] for plan in plans] for k in range(entries)
    ]
    order = [list(dict.fromkeys(e[0] for e in plan)) for plan in plans]
    steps = [mine_of([row[i] for row in order]) for i in range(n_lon - 1)]

    def lon_copy(src, dst, send, recv, d, target):
        return pltpu.make_async_remote_copy(
            src_ref=src, dst_ref=dst, send_sem=send, recv_sem=recv,
            device_id={"lat": my_lat, "lon": target}, device_id_type=MESH,
        )

    def route_copy(target):
        d = lax.rem(target - me + n_lon, n_lon)
        return lon_copy(routes.at[pl.ds(0, 1)], routes.at[pl.ds(d, 1)], route_send, route_recv, d, target)

    def bulk_copy(k):
        d = lax.rem(targets[k] - me + n_lon, n_lon)
        return pltpu.make_async_remote_copy(
            src_ref=outgoing.at[pl.ds(targets[k] * cap + halves[k] * piece, piece)],
            dst_ref=received.at[pl.ds(d * cap + halves[k] * piece, piece)],
            send_sem=bulk_send.at[int(k >= EARLY)], recv_sem=bulk_recv.at[d - 1],
            device_id={"lat": my_lat, "lon": targets[k]}, device_id_type=MESH,
        )

    def all_of(ref, send, recv):
        return pltpu.make_async_remote_copy(
            src_ref=ref, dst_ref=ref, send_sem=send, recv_sem=recv,
            device_id=peer(1), device_id_type=MESH,
        )

    chosen = [
        [jnp.maximum(v - 1, 0) for v in digits_of(0, target * blocks, lambda s, row: s)]
        for target in steps + [me]
    ]
    for load in loads[1:5]:
        load.wait()

    def fill(target, picks):
        for c, s in enumerate(picks):
            here = pl.ds(s, 1)
            amount = area[here, :] * frac[here, :] * mask[here, :].astype(jnp.float32)
            outgoing[target * cap + c] = flux[s] * amount

    bulk = [bulk_copy(k) for k in range(entries)]
    first_part = all_of(outgoing.at[pl.ds(0, EARLY * piece)], bulk_send.at[0], bulk_recv.at[0])
    rest_part = all_of(
        outgoing.at[pl.ds(0, (entries - EARLY) * piece)], bulk_send.at[1], bulk_recv.at[0]
    )

    def send(k):
        if any(holds[k]):
            @pl.when(mine_of(holds[k]) == 1)
            def _():
                pl.semaphore_wait(go, 1)

        waits = [
            first and plan[k][0] == top
            for z, (first, plan) in enumerate(zip(firsts[k], plans))
        ]
        if any(waits):
            @pl.when(mine_of(waits) == 1)
            def _():
                pl.semaphore_wait(top_in, 1)

        if all(firsts[k]):
            route_copy(targets[k]).start()
        elif any(firsts[k]):
            @pl.when(mine_of(firsts[k]) == 1)
            def _():
                route_copy(targets[k]).start()

        bulk[k].start()

    fill(steps[0], chosen[0])
    @pl.when(me < top)
    def _():
        pl.semaphore_wait(barrier, n_lat + n_lon - 3)

    @pl.when(kind == 0)
    def _():
        send(0)

    for target, picks in zip(steps[1:], chosen[1:-1]):
        fill(target, picks)

    @pl.when(kind == 0)
    def _():
        for k in range(1, entries):
            send(k)

    @pl.when(kind == 1)
    def _():
        for k in range(EARLY):
            send(k)

    for c, s in enumerate(chosen[-1]):
        here = pl.ds(s, 1)
        amount = area[here, :] * frac[here, :] * mask[here, :].astype(jnp.float32)
        received[c] = flux[s] * amount

    source_units = jnp.zeros((fields, width), jnp.int32)
    for s in range(blocks):
        here = pl.ds(s, 1)
        amount = area[here, :] * frac[here, :] * mask[here, :].astype(jnp.float32)
        units = (flux[s] * amount * quantum).astype(jnp.int32)
        for r in range(band):
            source_units += units[:, r * width : (r + 1) * width]

    for load in loads[5:]:
        load.wait()
    wetf[...] = wet[...].astype(jnp.float32)
    inverse[...] = wetf[...] / sea[...]
    area_units = jnp.zeros((8, width), jnp.int32)
    for i in range(rows // 8):
        part = pl.ds(i * 8, 8)
        area_units += (sea[part, :] * wetf[part, :] * quantum).astype(jnp.int32)

    held = [any(e[2] for e in plan) for plan in plans[n_lon:]]
    frees = mine_of(held + [False] * n_lon)
    if n_lat > 1 and any(held):
        @pl.when(frees == 1)
        def _():
            first_part.wait_send()
            pl.semaphore_signal(
                go, inc=1, device_id={"lat": my_lat + 1, "lon": me}, device_id_type=MESH
            )

    @pl.when(kind == 1)
    def _():
        for k in range(EARLY, entries):
            send(k)

    sub = lax.broadcasted_iota(jnp.int32, (8, lanes), 0)
    lane = lax.broadcasted_iota(jnp.int32, (8, lanes), 1)

    def placed(values, first):
        return sum(
            jnp.where(lane == sub + (first + i) * 8, v, 0.0) for i, v in enumerate(values)
        )

    firsts_row = placed(row_limbs(source_units) + row_limbs(area_units), 0)
    tally[pl.ds(0, 1), :] = jnp.sum(firsts_row, axis=0, keepdims=True)
    power = jnp.zeros((8, lanes), jnp.int32)
    power_row = jnp.zeros((1, lanes), jnp.int32)
    for f in range(fields):
        power = jnp.where(sub == f, exps[f], power)
        power_row = jnp.where(lane[:1] == f, exps[f], power_row)
    scaling = jnp.left_shift(jnp.ones_like(power), power).astype(jnp.float32)
    scaling_row = jnp.left_shift(jnp.ones_like(power_row), power_row).astype(jnp.float32)

    low = me * blocks
    slot_of = [jnp.int32(0)] * blocks
    near_first = sorted(range(n_lon), key=lambda d: min(d, n_lon - d))
    found = {}
    for d in near_first:
        if len(found) == 1:
            all_of(routes.at[pl.ds(1, n_lon - 1)], route_send, route_recv).wait_recv()
        found[d] = digits_of(d, low, lambda s, row: row)
        for c in range(cap):
            for n in range(blocks):
                slot_of[n] = jnp.where(found[d][c] == n + 1, d * cap + c, slot_of[n])

    def spread(base, recv):
        for offset in range(1, group):
            pltpu.make_async_remote_copy(
                src_ref=tally.at[pl.ds(base, 1)], dst_ref=tally.at[pl.ds(base + offset, 1)],
                send_sem=tally_send, recv_sem=recv,
                device_id=peer(offset), device_id_type=MESH,
            ).start()
        return all_of(tally.at[pl.ds(base + 1, group - 1)], tally_send, recv)

    early_rows = spread(0, early_recv)

    target_units = jnp.zeros((fields, width), jnp.int32)
    for d in near_first:
        if d:
            all_of(received.at[pl.ds(d * cap, cap)], bulk_send.at[0], bulk_recv.at[d - 1]).wait_recv()
        for c in range(cap):
            row = jnp.maximum(found[d][c] - 1, 0)
            for r in range(band):
                cover = wetf[pl.ds(row * band + r, 1), :]
                value = received[d * cap + c, :, r * width : (r + 1) * width]
                units = (cover * value * quantum).astype(jnp.int32)
                if not full:
                    units = units * jnp.minimum(found[d][c], 1)
                target_units += units

    tally[pl.ds(group, 1), :] = jnp.sum(placed(row_limbs(target_units), 0), axis=0, keepdims=True)
    late_rows = spread(group, late_recv)
    for n in range(blocks):
        slot = slot_of[n]
        for r in range(band):
            line = n * band + r
            value = received[slot, :, r * width : (r + 1) * width]
            ordered[pl.ds(line, fields, stride=rows), :] = value * inverse[line : line + 1, :]

    def taken(whole, i):
        return jnp.sum(jnp.where(lane == sub + i * 8, whole, 0.0), axis=1, keepdims=True)

    early_rows.wait_recv()
    whole = jnp.sum(tally[pl.ds(0, group), :], axis=0, keepdims=True)
    source = join(taken(whole, 0), taken(whole, 1))
    wet_upper, wet_lower = carry(taken(whole, 2), taken(whole, 3))
    wet_area = join(
        jnp.sum(wet_upper, axis=0, keepdims=True), jnp.sum(wet_lower, axis=0, keepdims=True)
    )
    coefs[0] = scaling
    share = scaling / wet_area
    total_ref[...] = join(whole, pltpu.roll(whole, lanes - 8, 1)) * scaling_row

    late_rows.wait_recv()
    whole = jnp.sum(tally[pl.ds(group, group), :], axis=0, keepdims=True)
    target = join(taken(whole, 0), taken(whole, 1))
    coefs[1] = (source - target) * share

    all_of(tally.at[pl.ds(0, 2 * (group - 1))], tally_send, late_recv).wait_send()
    all_of(routes.at[pl.ds(1, n_lon - 1)], route_send, route_recv).wait_send()

    @pl.when(frees == 0)
    def _():
        first_part.wait_send()

    rest_part.wait_send()


def finish(ordered, wetf, coefs, total_row, out_hbm, total_hbm, out, total, sems):
    fields = total.shape[0]
    rows = wetf.shape[0]
    total[...] = total_row[0, :fields]
    row = pltpu.make_async_copy(total, total_hbm, sems.at[0])
    row.start()
    for f in range(fields):
        here = pl.ds(f * rows, rows)
        out[here, :] = ordered[here, :] * coefs[0, f : f + 1, :] + wetf[...] * coefs[1, f : f + 1, :]
        pltpu.make_async_copy(out.at[here], out_hbm.at[here], sems.at[1]).start()
    row.wait()
    pltpu.make_async_copy(out, out_hbm, sems.at[1]).wait()


def solution(mesh):
    n_lat, n_lon = mesh.shape["lat"], mesh.shape["lon"]

    def body(ice_flux, ice_frac, ice_mask, ice_area, route, ocean_area, ocean_wet, exponent):
        blocks, fields, cells = ice_flux.shape[1:]
        rows, width = ocean_area.shape
        cap = max(2, blocks // n_lon)
        group = n_lat * n_lon
        anywhere = pl.BlockSpec(memory_space=pl.ANY)
        vmem = pl.BlockSpec(memory_space=pltpu.VMEM)
        dma = pltpu.SemaphoreType.DMA
        near = pl.pallas_call(
            functools.partial(kernel, n_lat, n_lon, cap),
            out_shape=(
                pltpu.VMEM((fields * rows, width), jnp.float32),
                pltpu.VMEM((rows, width), jnp.float32),
                pltpu.VMEM((2, fields, lanes), jnp.float32),
                pltpu.VMEM((1, lanes), jnp.float32),
            ),
            in_specs=[anywhere] * 8,
            out_specs=(vmem,) * 4,
            scratch_shapes=[
                pltpu.VMEM((blocks, fields, cells), jnp.float32),
                pltpu.VMEM((blocks, cells), jnp.float32),
                pltpu.VMEM((blocks, cells), jnp.int32),
                pltpu.VMEM((blocks, cells), jnp.float32),
                pltpu.VMEM((rows, width), jnp.float32),
                pltpu.VMEM((rows, width), jnp.int32),
                pltpu.VMEM((rows, width), jnp.float32),
                pltpu.VMEM((n_lon * cap, fields, cells), jnp.float32),
                pltpu.VMEM((n_lon * cap, fields, cells), jnp.float32),
                pltpu.SMEM((n_lon, blocks), jnp.int32),
                pltpu.SMEM((fields,), jnp.int32),
                pltpu.VMEM((2 * group, lanes), jnp.float32),
                dma((8,)),
                dma, dma, dma((2,)), dma((n_lon - 1,)), dma, dma, dma,
                pltpu.SemaphoreType.REGULAR, pltpu.SemaphoreType.REGULAR,
            ],
            compiler_params=pltpu.CompilerParams(collective_id=0, has_side_effects=True),
        )(
            ice_flux[0], ice_frac[0], ice_mask[0], ice_area[0],
            route, ocean_area, ocean_wet, exponent,
        )
        flux_out, total = pl.pallas_call(
            finish,
            out_shape=(
                jax.ShapeDtypeStruct((fields * rows, width), jnp.float32),
                jax.ShapeDtypeStruct((fields,), jnp.float32),
            ),
            in_specs=[vmem] * 4,
            out_specs=(anywhere, anywhere),
            scratch_shapes=[
                pltpu.VMEM((fields * rows, width), jnp.float32),
                pltpu.VMEM((fields,), jnp.float32),
                dma((2,)),
            ],
        )(*(pltpu.with_memory_space_constraint(x, pltpu.VMEM) for x in near))
        return flux_out.reshape(fields, rows, width), total

    placed = (
        P(("member", "lat"), "lon", None, None),
        P(("member", "lat"), "lon", None),
        P(("member", "lat"), "lon", None),
        P(("member", "lat"), "lon", None),
        P(("member", "lat"), "lon"),
        P(("member", "lat"), "lon"),
        P(("member", "lat"), "lon"),
        P(),
    )
    return jax.shard_map(
        body,
        mesh=mesh,
        in_specs=placed,
        out_specs=(P(None, ("member", "lat"), "lon"), P("member")),
        check_vma=False,
    )
```

time: 17.8 us -> 15.9 us (0.89)
  Pallas kernels: 17 us -> 15.1 us
    pallas_call x1, Pallas kernels: 16.2 us -> 14.3 us  [body(): pl.pallas_call(functools.partial(kernel, n_lat, n_lon, cap), out_shape=(p...]
where the time goes in v2:
time: 15.9 us; the launch traced here: 15.7 us
  Pallas kernels  15.1 us (95%)
  between operations  0.64 us (4%)
    pallas_call x1, Pallas kernels, body(): pl.pallas_call(functools.partial(kernel, n_lat, n_lon, cap), out_shape=(p...  14.3 us
    pallas_call x1, Pallas kernels, body(): pl.pallas_call(finish, out_shape=(jax.ShapeDtypeStruct((fields * rows, wi...  0.71 us

profile of v2, /device:TPU:0, one launch (start us, length us, event | category | flops | bytes accessed | tf_op | source)
XLA Modules:
  0.0 15.7 jit_solution(10033210743200269511)
XLA Ops:
  0.6 14.3 %shard_map.95 = (f32[512,128]{1,0:T(8,128)S(1)}, f32[64,128]{1,0:T(8,128)S(1)}, f32[2,8,128]{2,1,0:T(8,128)S(1)}, f32[1,128]{1,0:T(1,128)S(1)}) custom-call(f32[16,8,512]{2,1,0:T(8,128)} %bitcast.5, f32[16,512]{1,0:T(8,128)} %bitcast.6, s32[16,512]{1,0:T(8,128)} %bitcast.7, f32[16,512]{1,0:T(8,128)} %bitcast.8, s32[1,16]{1,0:T(1,128)} %route_hbm.1, ...), custom_call_target="tpu_custom_call" | custom-call | tf_op jit(solution)/shard_map/pallas_call | solution.py:392
  15.0 0.7 %shard_map.96 = (f32[512,128]{1,0:T(8,128)}, f32[8]{0:T(128)}) custom-call(f32[512,128]{1,0:T(8,128)S(1)} %get-tuple-element.8.ordered, f32[64,128]{1,0:T(8,128)S(1)} %get-tuple-element.9.wetf, f32[2,8,128]{2,1,0:T(8,128)S(1)} %get-tuple-element.10.coefs, f32[1,128]{1,0:T(1,128)S(1)} %get-tuple-element.11.total_row), custom_call_target="tpu_custom_call" | custom-call | tf_op jit(solution)/shard_map/pallas_call | solution.py:424

commit v3 on v2

--- a/solution.py
+++ b/solution.py
@@ -66,12 +66,13 @@
     flux_hbm, frac_hbm, mask_hbm, area_hbm, route_hbm, sea_hbm, wet_hbm, exp_hbm,
     ordered, wetf, coefs, total_ref,
     flux, frac, mask, area, sea, wet, inverse, outgoing, received, routes, exps, tally,
-    in_sem, route_send, route_recv, bulk_send, bulk_recv, tally_send, early_recv, late_recv, top_in, go,
+    in_sem, route_recv, bulk_recv, early_recv, late_recv, top_in, go,
 ):
     blocks, fields, cells = flux.shape
     rows, width = sea.shape
     band = cells // width
     bits = blocks.bit_length()
+    route_send, tally_send, bulk_send = in_sem.at[1], in_sem.at[2], [in_sem.at[3], in_sem.at[4]]
     digit = (1 << bits) - 1
     full = cap * n_lon == blocks
     group = n_lat * n_lon
@@ -159,7 +160,7 @@
         return pltpu.make_async_remote_copy(
             src_ref=outgoing.at[pl.ds(targets[k] * cap + halves[k] * piece, piece)],
             dst_ref=received.at[pl.ds(d * cap + halves[k] * piece, piece)],
-            send_sem=bulk_send.at[int(k >= EARLY)], recv_sem=bulk_recv.at[d - 1],
+            send_sem=bulk_send[int(k >= EARLY)], recv_sem=bulk_recv.at[d - 1],
             device_id={"lat": my_lat, "lon": targets[k]}, device_id_type=MESH,
         )
 
@@ -183,9 +184,9 @@
             outgoing[target * cap + c] = flux[s] * amount
 
     bulk = [bulk_copy(k) for k in range(entries)]
-    first_part = all_of(outgoing.at[pl.ds(0, EARLY * piece)], bulk_send.at[0], bulk_recv.at[0])
+    first_part = all_of(outgoing.at[pl.ds(0, EARLY * piece)], bulk_send[0], bulk_recv.at[0])
     rest_part = all_of(
-        outgoing.at[pl.ds(0, (entries - EARLY) * piece)], bulk_send.at[1], bulk_recv.at[0]
+        outgoing.at[pl.ds(0, (entries - EARLY) * piece)], bulk_send[1], bulk_recv.at[0]
     )
 
     def send(k):
@@ -302,12 +303,14 @@
                 slot_of[n] = jnp.where(found[d][c] == n + 1, d * cap + c, slot_of[n])
 
     def spread(base, recv):
-        for offset in range(1, group):
-            pltpu.make_async_remote_copy(
-                src_ref=tally.at[pl.ds(base, 1)], dst_ref=tally.at[pl.ds(base + offset, 1)],
-                send_sem=tally_send, recv_sem=recv,
-                device_id=peer(offset), device_id_type=MESH,
-            ).start()
+        for lon in range(n_lon):
+            for lat in range(n_lat):
+                offset = lax.rem(lat - my_lat + n_lat, n_lat) * n_lon + lax.rem(lon - me + n_lon, n_lon)
+                pl.when(offset > 0)(pltpu.make_async_remote_copy(
+                    src_ref=tally.at[pl.ds(base, 1)], dst_ref=tally.at[pl.ds(base + offset, 1)],
+                    send_sem=tally_send, recv_sem=recv,
+                    device_id={"lat": jnp.int32(lat), "lon": jnp.int32(lon)}, device_id_type=MESH,
+                ).start)
         return all_of(tally.at[pl.ds(base + 1, group - 1)], tally_send, recv)
 
     early_rows = spread(0, early_recv)
@@ -315,7 +318,7 @@
     target_units = jnp.zeros((fields, width), jnp.int32)
     for d in near_first:
         if d:
-            all_of(received.at[pl.ds(d * cap, cap)], bulk_send.at[0], bulk_recv.at[d - 1]).wait_recv()
+            all_of(received.at[pl.ds(d * cap, cap)], bulk_send[0], bulk_recv.at[d - 1]).wait_recv()
         for c in range(cap):
             row = jnp.maximum(found[d][c] - 1, 0)
             for r in range(band):
@@ -333,7 +336,7 @@
         for r in range(band):
             line = n * band + r
             value = received[slot, :, r * width : (r + 1) * width]
-            ordered[pl.ds(line, fields, stride=rows), :] = value * inverse[line : line + 1, :]
+            ordered[pl.ds(line, fields, stride=rows), :] = value * (inverse[line : line + 1, :] * scaling)
 
     def taken(whole, i):
         return jnp.sum(jnp.where(lane == sub + i * 8, whole, 0.0), axis=1, keepdims=True)
@@ -345,14 +348,13 @@
     wet_area = join(
         jnp.sum(wet_upper, axis=0, keepdims=True), jnp.sum(wet_lower, axis=0, keepdims=True)
     )
-    coefs[0] = scaling
     share = scaling / wet_area
     total_ref[...] = join(whole, pltpu.roll(whole, lanes - 8, 1)) * scaling_row
 
     late_rows.wait_recv()
     whole = jnp.sum(tally[pl.ds(group, group), :], axis=0, keepdims=True)
     target = join(taken(whole, 0), taken(whole, 1))
-    coefs[1] = (source - target) * share
+    coefs[...] = jnp.broadcast_to((source - target) * share, (fields, lanes))
 
     all_of(tally.at[pl.ds(0, 2 * (group - 1))], tally_send, late_recv).wait_send()
     all_of(routes.at[pl.ds(1, n_lon - 1)], route_send, route_recv).wait_send()
@@ -372,7 +374,7 @@
     row.start()
     for f in range(fields):
         here = pl.ds(f * rows, rows)
-        out[here, :] = ordered[here, :] * coefs[0, f : f + 1, :] + wetf[...] * coefs[1, f : f + 1, :]
+        out[here, :] = ordered[here, :] + wetf[...] * coefs[f : f + 1, :]
         pltpu.make_async_copy(out.at[here], out_hbm.at[here], sems.at[1]).start()
     row.wait()
     pltpu.make_async_copy(out, out_hbm, sems.at[1]).wait()
@@ -394,7 +396,7 @@
             out_shape=(
                 pltpu.VMEM((fields * rows, width), jnp.float32),
                 pltpu.VMEM((rows, width), jnp.float32),
-                pltpu.VMEM((2, fields, lanes), jnp.float32),
+                pltpu.VMEM((fields, lanes), jnp.float32),
                 pltpu.VMEM((1, lanes), jnp.float32),
             ),
             in_specs=[anywhere] * 8,
@@ -413,7 +415,7 @@
                 pltpu.SMEM((fields,), jnp.int32),
                 pltpu.VMEM((2 * group, lanes), jnp.float32),
                 dma((8,)),
-                dma, dma, dma((2,)), dma((n_lon - 1,)), dma, dma, dma,
+                dma, dma((n_lon - 1,)), dma, dma,
                 pltpu.SemaphoreType.REGULAR, pltpu.SemaphoreType.REGULAR,
             ],
             compiler_params=pltpu.CompilerParams(collective_id=0, has_side_effects=True),

time: 15.9 us -> 15.8 us (level)
  no operation moved by 1% of the time
where the time goes in v3:
time: 15.8 us; the launch traced here: 15.6 us
  Pallas kernels  15 us (95%)
  between operations  0.64 us (4%)
    pallas_call x1, Pallas kernels, body(): pl.pallas_call(functools.partial(kernel, n_lat, n_lon, cap), out_shape=(p...  14.3 us
    pallas_call x1, Pallas kernels, body(): pl.pallas_call(finish, out_shape=(jax.ShapeDtypeStruct((fields * rows, wi...  0.72 us

profile of v3, /device:TPU:0, one launch (start us, length us, event | category | flops | bytes accessed | tf_op | source)
XLA Modules:
  0.0 15.6 jit_solution(17814986518658010478)
XLA Ops:
  0.6 14.3 %shard_map.95 = (f32[512,128]{1,0:T(8,128)S(1)}, f32[64,128]{1,0:T(8,128)S(1)}, f32[8,128]{1,0:T(8,128)S(1)}, f32[1,128]{1,0:T(1,128)S(1)}) custom-call(f32[16,8,512]{2,1,0:T(8,128)} %bitcast.5, f32[16,512]{1,0:T(8,128)} %bitcast.6, s32[16,512]{1,0:T(8,128)} %bitcast.7, f32[16,512]{1,0:T(8,128)} %bitcast.8, s32[1,16]{1,0:T(1,128)} %route_hbm.1, ...), custom_call_target="tpu_custom_call" | custom-call | tf_op jit(solution)/shard_map/pallas_call | solution.py:394
  14.9 0.7 %shard_map.96 = (f32[512,128]{1,0:T(8,128)}, f32[8]{0:T(128)}) custom-call(f32[512,128]{1,0:T(8,128)S(1)} %get-tuple-element.8.ordered, f32[64,128]{1,0:T(8,128)S(1)} %get-tuple-element.9.wetf, f32[8,128]{1,0:T(8,128)S(1)} %get-tuple-element.10.coefs, f32[1,128]{1,0:T(1,128)S(1)} %get-tuple-element.11.total_row), custom_call_target="tpu_custom_call" | custom-call | tf_op jit(solution)/shard_map/pallas_call | solution.py:426

commit v4 on v3

--- a/solution.py
+++ b/solution.py
@@ -36,7 +36,7 @@
         (2, 3, 0, 1, 6, 7),
         (2, 3, 0, 1, 4, 5),
         (2, 4, 6, -8, 5, 3),
-        (4, 5, 6, -8, 0, 1),
+        (0, 4, 5, 6, -8, 1),
         (2, 0, 1, 3, 6, 7),
         (2, 0, 1, 3, 4, 5),
     ),

time: 15.8 us -> 15.8 us (level)
  no operation moved by 1% of the time
where the time goes in v4:
time: 15.8 us; the launch traced here: 15.6 us
  Pallas kernels  15 us (95%)
  between operations  0.64 us (4%)
    pallas_call x1, Pallas kernels, body(): pl.pallas_call(functools.partial(kernel, n_lat, n_lon, cap), out_shape=(p...  14.3 us
    pallas_call x1, Pallas kernels, body(): pl.pallas_call(finish, out_shape=(jax.ShapeDtypeStruct((fields * rows, wi...  0.72 us

profile of v4, /device:TPU:0, one launch (start us, length us, event | category | flops | bytes accessed | tf_op | source)
XLA Modules:
  0.0 15.6 jit_solution(16866945105357032161)
XLA Ops:
  0.6 14.3 %shard_map.95 = (f32[512,128]{1,0:T(8,128)S(1)}, f32[64,128]{1,0:T(8,128)S(1)}, f32[8,128]{1,0:T(8,128)S(1)}, f32[1,128]{1,0:T(1,128)S(1)}) custom-call(f32[16,8,512]{2,1,0:T(8,128)} %bitcast.5, f32[16,512]{1,0:T(8,128)} %bitcast.6, s32[16,512]{1,0:T(8,128)} %bitcast.7, f32[16,512]{1,0:T(8,128)} %bitcast.8, s32[1,16]{1,0:T(1,128)} %route_hbm.1, ...), custom_call_target="tpu_custom_call" | custom-call | tf_op jit(solution)/shard_map/pallas_call | solution.py:394
  14.9 0.7 %shard_map.96 = (f32[512,128]{1,0:T(8,128)}, f32[8]{0:T(128)}) custom-call(f32[512,128]{1,0:T(8,128)S(1)} %get-tuple-element.8.ordered, f32[64,128]{1,0:T(8,128)S(1)} %get-tuple-element.9.wetf, f32[8,128]{1,0:T(8,128)S(1)} %get-tuple-element.10.coefs, f32[1,128]{1,0:T(1,128)S(1)} %get-tuple-element.11.total_row), custom_call_target="tpu_custom_call" | custom-call | tf_op jit(solution)/shard_map/pallas_call | solution.py:426
